TPU v7x, 32 devices: a whole 2x2x4 slice. The times are simulated.
32 devices in a mesh: groups: 2 (over y), rows: 4 (over z), cols: 2 (over x), sub: 2 (over core).
Axes of the slice: x: 2, y: 2, z: 4, core: 2. Of those that a mesh axis runs over, the one named last changes fastest.
Arguments:
- stored_vectors: bfloat16 [3072, 8192], P(('cols', 'sub'), ('groups', 'rows')), parts along dimension 1, may hold values from -0.59765625 to 0.59765625
- previous_columns: bfloat16 [8192, 256], P(('groups', 'rows', 'cols', 'sub')), parts along dimension 0, may hold values from -3 to 3
- pivots: int32 [512], P('groups'), parts along dimension 0, may hold values from 0 to 4095, as said below
- diagonal: float32 [8192], P(('groups', 'rows', 'cols', 'sub')), parts along dimension 0, may hold values from 2 to 32
- ket_blocks: bfloat16 [128, 128, 256], P(('groups', 'rows', 'cols', 'sub')), parts along dimension 0, may hold values from -6 to 6
- shell_tags: int32 [128, 128], P(('groups', 'rows', 'cols', 'sub')), parts along dimension 0, may hold values from 0 to 3
- target_blocks: int32 [32, 4], P('groups'), parts along dimension 0, may hold values from 0 to 31, as said below
- block_counts: int32 [32], P('groups'), parts along dimension 0, may hold values from 0 to 4, as said below
- shell_norms: float32 [4], replicated, may hold values from 0.5 to 2
Outputs:
- new_vectors: bfloat16 [8192, 256], P(('groups', 'rows', 'cols', 'sub')), parts along dimension 0
- diag_out: float32 [8192], P(('groups', 'rows', 'cols', 'sub')), parts along dimension 0
- next_columns: bfloat16 [8192, 256], P(('groups', 'rows', 'cols', 'sub')), parts along dimension 0
There are 2 independent parts, one for each index of `groups`. A program takes and returns all parts, laid end to end along the dimension named above; an argument that names none is the same for every part. Nothing has to cross between parts.
Inputs may be any that keep to these rules, and one draw needn't show every extreme that they name: `pivots`: 256 distinct AO pairs. `target_blocks`: the used slots of all owners name every block of the 32 blocks exactly once; a used slot's block lies on a device with the owner's cols and sub indices (blocks g * 2 to g * 2 + 1 lie on the device of linear index g, rows slowest; owner o is the device of linear index o). At most 1 of one owner's used slots go to one device, and some owner reaches that in every draw. Entries of unused slots are arbitrary blocks. `block_counts`: some owner uses all 4 slots in every draw.
All inputs are finite; a program needn't handle non-finite values.
Results may differ from a plain program's by a relative error of at most 0.0004.
Values may be sent and summed in bfloat16 or wider, within the bound.
A program may use at most 64 MiB of HBM per device.

v0:
```python
import functools

import jax
import jax.numpy as jnp
from jax import lax
from jax.experimental import pallas as pl
from jax.experimental.pallas import tpu as pltpu
from jax.sharding import PartitionSpec as P

MESH = pl.DeviceIdType.MESH
LANES = 128


def column_of(row):
    return jnp.transpose(jnp.broadcast_to(row, (LANES, row.shape[1])))


def kernel(
    sizes,
    vec_hbm, prev_hbm, piv_ref, diag_ref, ket_hbm, tags_ref, targets_ref, counts_ref, norms_ref,
    new_ref, diag_out_ref, next_ref,
    vec, prev, ket, hot, own, fwd_r, fwd_l, from_l, from_r,
    pivot_t, prev_t, sub_out, sub_in, mine, col_out, col_in, scaled_t,
    stage, landed, pd_z, pd_s, pd_c, pd_own_s, pd_own_c,
    load_sem, zr_send, zl_send, l_recv, r_recv, sub_send, sub_recv, col_send, col_recv,
    ket_send, ket_recv, pdz_send, pdz_recv, pds_send, pds_recv, pdc_send, pdc_recv,
):
    n_rows, n_cols, n_sub, hop_lead = sizes
    z, x, s = lax.axis_index("rows"), lax.axis_index("cols"), lax.axis_index("sub")
    column_size = n_cols * n_sub
    column = x * n_sub + s
    device = z * column_size + column
    slot_count, block_rows, batch = ket_hbm.shape
    rows_here = prev_hbm.shape[0]
    per_device = rows_here // block_rows
    width, band_rows = vec_hbm.shape
    z_chunks, z_rows = own.shape[0], own.shape[1]
    m_chunks, m_rows = mine.shape[0], mine.shape[1]
    per_m = m_rows // z_rows

    load_ket = pltpu.make_async_copy(ket_hbm, ket, load_sem.at[0])
    load_vec = pltpu.make_async_copy(vec_hbm, vec, load_sem.at[1])
    load_prev = pltpu.make_async_copy(prev_hbm, prev, load_sem.at[2])
    load_ket.start()
    load_vec.start()
    load_prev.start()

    barrier = pltpu.get_barrier_semaphore()
    for name, here, count in (("rows", z, n_rows), ("cols", x, n_cols), ("sub", s, n_sub)):
        for d in range(1, count):
            pl.semaphore_signal(
                barrier, inc=1, device_id={name: lax.rem(here + d, count)}, device_id_type=MESH
            )

    piv_col = column_of(piv_ref[...].astype(jnp.float32)).astype(jnp.int32) - z * band_rows
    lane = lax.broadcasted_iota(jnp.int32, (batch, LANES), 1)
    for t in range(band_rows // LANES):
        hot[:, t * LANES:(t + 1) * LANES] = (piv_col == lane + t * LANES).astype(
            jnp.float32).astype(jnp.bfloat16)

    diag_col = column_of(diag_ref[...])
    row = lax.broadcasted_iota(jnp.int32, (rows_here, LANES), 0) + device * rows_here
    for h in range(batch // LANES):
        cut = slice(h * LANES, (h + 1) * LANES)
        share = jnp.sum(jnp.where(piv_ref[:, cut] == row, diag_col, 0.0), axis=0, keepdims=True)
        pd_z[n_rows, :, cut] = jnp.broadcast_to(share, (8, LANES))

    tags = tags_ref[...]
    factor = jnp.zeros(tags.shape, jnp.float32)
    for kind in range(norms_ref.shape[0]):
        factor = jnp.where(tags == kind, norms_ref[kind], factor)
    load_ket.wait()
    for slot in range(slot_count):
        scale = column_of(factor[slot:slot + 1, :])
        for h in range(batch // LANES):
            part = (slot, slice(None), slice(h * LANES, (h + 1) * LANES))
            ket[part] = (ket[part].astype(jnp.float32) * scale).astype(jnp.bfloat16)
    used = counts_ref[device]

    def stage_for(band):
        low = (band * column_size + column) * per_device
        chosen = jnp.int32(0)
        for slot in range(slot_count):
            target = targets_ref[slot, device]
            fits = (slot < used) & (target >= low) & (target < low + per_device)
            chosen = jnp.where(fits, jnp.int32(slot), chosen)
        return ket[chosen]

    landed[z] = stage_for(z)
    for d in range(1, n_rows):
        stage[d] = stage_for(lax.rem(z + d, n_rows))

    def ket_copy(d):
        return pltpu.make_async_remote_copy(
            src_ref=stage.at[d], dst_ref=landed.at[z], send_sem=ket_send.at[d],
            recv_sem=ket_recv.at[z], device_id={"rows": lax.rem(z + d, n_rows)},
            device_id_type=MESH)

    pl.semaphore_wait(barrier, n_rows + n_cols + n_sub - 3)

    def pd_copies(src, dst, send, recv, name, here, count):
        return [pltpu.make_async_remote_copy(
            src_ref=src, dst_ref=dst.at[here], send_sem=send.at[d], recv_sem=recv.at[here],
            device_id={name: lax.rem(here + d, count)}, device_id_type=MESH)
            for d in range(1, count)]

    pdz = pd_copies(pd_z.at[n_rows], pd_z, pdz_send, pdz_recv, "rows", z, n_rows)
    pds = pd_copies(pd_own_s, pd_s, pds_send, pds_recv, "sub", s, n_sub)
    pdc = pd_copies(pd_own_c, pd_c, pdc_send, pdc_recv, "cols", x, n_cols)
    for c in pdz:
        c.start()

    inner = (z > 0) & (z < n_rows - 1)

    @pl.when(inner)
    def _():
        for d in range(1, n_rows):
            ket_copy(d).start()

    def z_copy(src, dst, send, recv, q, dz):
        return pltpu.make_async_remote_copy(
            src_ref=src.at[q], dst_ref=dst.at[q], send_sem=send.at[q], recv_sem=recv.at[q],
            device_id={"rows": lax.rem(z + dz + n_rows, n_rows)}, device_id_type=MESH)

    def arrived(dst, sem):
        pltpu.make_async_remote_copy(
            src_ref=dst, dst_ref=dst, send_sem=sem, recv_sem=sem,
            device_id={"sub": lax.rem(s + 1, n_sub)}, device_id_type=MESH).wait_recv()

    load_vec.wait()
    piece = min(LANES, batch)
    in_piece = piece // z_rows
    for p in range(batch // piece):
        got = lax.dot_general(
            hot[p * piece:(p + 1) * piece, :], vec[...], (((1,), (1,)), ((), ())),
            preferred_element_type=jnp.float32).astype(jnp.bfloat16)
        got = got.reshape(in_piece, z_rows, width)
        own[p * in_piece:(p + 1) * in_piece] = got

        @pl.when(z == 0)
        def _():
            fwd_r[p * in_piece:(p + 1) * in_piece] = got
            for q in range(p * in_piece, (p + 1) * in_piece):
                z_copy(own, from_l, zr_send, l_recv, q, 1).start()

        @pl.when(z == n_rows - 1)
        def _():
            for q in range(p * in_piece, (p + 1) * in_piece):
                z_copy(own, from_r, zl_send, r_recv, q, -1).start()

    def pd_total(first, dst, recv, here, count):
        total = first[...]
        for d in range(1, count):
            other = lax.rem(here + d, count)
            arrived(dst.at[other], recv.at[other])
            total = total + dst[other]
        return total

    load_prev.wait()
    prev_t[...] = jnp.transpose(prev[...].astype(jnp.float32))

    tilt = jnp.where(inner, hop_lead * (2 * z - (n_rows - 1)), 0)
    wait_l = jnp.clip(tilt, 0, z_chunks)
    wait_r = jnp.clip(-tilt, 0, z_chunks)
    lag = jnp.maximum(wait_l, wait_r)
    most_lag = min(z_chunks, hop_lead * max(n_rows - 3, 0))

    def sub_copy(m, d):
        return pltpu.make_async_remote_copy(
            src_ref=sub_out.at[m, d], dst_ref=sub_in.at[m, s], send_sem=sub_send.at[m, d],
            recv_sem=sub_recv.at[m, s], device_id={"sub": lax.rem(s + d, n_sub)},
            device_id_type=MESH)

    def col_copy(m, d):
        return pltpu.make_async_remote_copy(
            src_ref=col_out.at[m, d], dst_ref=col_in.at[m, x], send_sem=col_send.at[m, d],
            recv_sem=col_recv.at[m, x], device_id={"cols": lax.rem(x + d, n_cols)},
            device_id_type=MESH)

    def block_dot(pivot_rows_t, col, sub):
        at = pl.multiple_of((col * n_sub + sub) * rows_here, LANES)
        return jnp.dot(
            pivot_rows_t, vec[:, pl.ds(at, rows_here)], preferred_element_type=jnp.float32)

    def multiply(m):
        rows = pl.ds(m * per_m, per_m)

        @pl.when(z < n_rows - 1)
        def _():
            pivot_t[rows] = fwd_r[rows] + from_r[rows]

        @pl.when(z == n_rows - 1)
        def _():
            pivot_t[rows] = fwd_r[rows]

        pt = pivot_t[rows].reshape(m_rows, width)
        for d in range(1, n_sub):
            for c in range(n_cols):
                sub_out[m, d, c] = block_dot(
                    pt, lax.rem(x + c, n_cols), lax.rem(s + d, n_sub))
            sub_copy(m, d).start()
        for c in range(1, n_cols):
            col_out[m, c] = block_dot(pt, lax.rem(x + c, n_cols), s)
        mine[m] = block_dot(pt, x, s)

    def reduce_chip(m):
        for d in range(1, n_sub):
            other = lax.rem(s + d, n_sub)
            arrived(sub_in.at[m, other], sub_recv.at[m, other])
        for c in range(1, n_cols):
            total = col_out[m, c]
            for d in range(1, n_sub):
                total = total + sub_in[m, lax.rem(s + d, n_sub), c]
            col_out[m, c] = total
            col_copy(m, c).start()
        total = mine[m]
        for d in range(1, n_sub):
            total = total + sub_in[m, lax.rem(s + d, n_sub), 0]
        mine[m] = total

    steps = most_lag + z_chunks + 1

    def step(t, carry):
        q_l, q_r, q_m = t - wait_l, t - wait_r, t - lag

        @pl.when((z > 0) & (q_l >= 0) & (q_l < z_chunks))
        def _():
            z_copy(fwd_r, from_l, zr_send, l_recv, q_l, 1).wait_recv()
            fwd_r[q_l] = from_l[q_l] + own[q_l]

            @pl.when(z < n_rows - 1)
            def _():
                z_copy(fwd_r, from_l, zr_send, l_recv, q_l, 1).start()

        @pl.when((z < n_rows - 1) & (q_r >= 0) & (q_r < z_chunks))
        def _():
            z_copy(fwd_l, from_r, zl_send, r_recv, q_r, -1).wait_recv()

            @pl.when(z > 0)
            def _():
                fwd_l[q_r] = from_r[q_r] + own[q_r]
                z_copy(fwd_l, from_r, zl_send, r_recv, q_r, -1).start()

        @pl.when(jnp.logical_not(inner) & (q_m == z_chunks - 2))
        def _():
            for d in range(1, n_rows):
                ket_copy(d).start()

        @pl.when((q_m >= per_m) & (q_m <= z_chunks) & (lax.rem(q_m, per_m) == 0))
        def _():
            reduce_chip(q_m // per_m - 1)

        @pl.when((q_m >= 0) & (q_m < z_chunks) & (lax.rem(q_m, per_m) == per_m - 1))
        def _():
            multiply(q_m // per_m)

        @pl.when(t == z_chunks // 2)
        def _():
            pd_own_s[...] = pd_total(pd_z.at[n_rows], pd_z, pdz_recv, z, n_rows)
            for c in pds:
                c.start()

        @pl.when(t == z_chunks - 1)
        def _():
            pd_own_c[...] = pd_total(pd_own_s, pd_s, pds_recv, s, n_sub)
            for c in pdc:
                c.start()

        return carry

    lax.fori_loop(0, steps, step, 0)

    pivot_diag = pd_total(pd_own_c, pd_c, pdc_recv, x, n_cols)
    inverse = 1.0 / jnp.sqrt(column_of(pivot_diag[0:1, :]))
    total_sq = jnp.zeros((1, rows_here), jnp.float32)
    per_t = max(LANES // m_rows, 1)
    for m in range(m_chunks):
        if m == m_chunks - 1:
            for d in range(1, n_rows):
                other = lax.rem(z + d, n_rows)
                arrived(landed.at[other], ket_recv.at[other])
            for place in range(per_device):
                block = device * per_device + place
                source = jnp.int32(0)
                for band in range(n_rows):
                    owner = band * column_size + column
                    for slot in range(slot_count):
                        fits = (slot < counts_ref[owner]) & (targets_ref[slot, owner] == block)
                        source = jnp.where(fits, jnp.int32(band), source)
                next_ref[place * block_rows:(place + 1) * block_rows, :] = landed[source]
        total = mine[m]
        for c in range(1, n_cols):
            other = lax.rem(x + c, n_cols)
            arrived(col_in.at[m, other], col_recv.at[m, other])
            total = total + col_in[m, other]
        rows = slice(m * m_rows, (m + 1) * m_rows)
        for h in range(rows_here // LANES):
            cut = slice(h * LANES, (h + 1) * LANES)
            scaled_t[rows, cut] = (prev_t[rows, cut] - total[:, cut]) * inverse[rows, :]
        scaled = scaled_t[rows, :]
        total_sq = total_sq + jnp.sum(scaled * scaled, axis=0, keepdims=True)
        if (m + 1) % per_t == 0:
            done = slice((m + 1 - per_t) * m_rows, (m + 1) * m_rows)
            new_ref[:, done] = jnp.transpose(scaled_t[done, :]).astype(jnp.bfloat16)
    diag_out_ref[...] = diag_ref[...] - total_sq

    for c in pdz + pds + pdc:
        c.wait_send()
    for d in range(1, n_rows):
        ket_copy(d).wait_send()

    @pl.when(z < n_rows - 1)
    def _():
        for q in range(z_chunks):
            z_copy(own, from_l, zr_send, l_recv, q, 1).wait_send()

    @pl.when(z > 0)
    def _():
        for q in range(z_chunks):
            z_copy(own, from_r, zl_send, r_recv, q, -1).wait_send()

    for m in range(m_chunks):
        for d in range(1, n_sub):
            sub_copy(m, d).wait_send()
        for c in range(1, n_cols):
            col_copy(m, c).wait_send()


def body(mesh_sizes, vectors, previous, pivots, diagonal, ket_blocks, tags, targets, counts, norms):
    n_rows, n_cols, n_sub = mesh_sizes
    width, band_rows = vectors.shape
    rows_here, batch = previous.shape
    slot_count, block_rows, _ = ket_blocks.shape
    z_chunks, m_chunks, hop_lead = 8, 4, 3
    z_rows, m_rows = batch // z_chunks, batch // m_chunks
    f32, bf16, dma = jnp.float32, jnp.bfloat16, pltpu.SemaphoreType.DMA
    line = pltpu.VMEM((z_chunks, z_rows, width), bf16)
    small = pltpu.VMEM((8, batch), f32)
    scratch = [
        pltpu.VMEM(vectors.shape, bf16), pltpu.VMEM(previous.shape, bf16),
        pltpu.VMEM(ket_blocks.shape, bf16), pltpu.VMEM((batch, band_rows), bf16),
        line, line, line, line, line, line,
        pltpu.VMEM((batch, rows_here), f32),
        pltpu.VMEM((m_chunks, n_sub, n_cols, m_rows, rows_here), f32),
        pltpu.VMEM((m_chunks, n_sub, n_cols, m_rows, rows_here), f32),
        pltpu.VMEM((m_chunks, m_rows, rows_here), f32),
        pltpu.VMEM((m_chunks, n_cols, m_rows, rows_here), f32),
        pltpu.VMEM((m_chunks, n_cols, m_rows, rows_here), f32),
        pltpu.VMEM((batch, rows_here), f32),
        pltpu.VMEM((n_rows, block_rows, batch), bf16),
        pltpu.VMEM((n_rows, block_rows, batch), bf16),
        pltpu.VMEM((n_rows + 1, 8, batch), f32), pltpu.VMEM((n_sub, 8, batch), f32),
        pltpu.VMEM((n_cols, 8, batch), f32), small, small,
        dma((3,)), dma((z_chunks,)), dma((z_chunks,)), dma((z_chunks,)), dma((z_chunks,)),
        dma((m_chunks, n_sub)), dma((m_chunks, n_sub)),
        dma((m_chunks, n_cols)), dma((m_chunks, n_cols)),
        dma((n_rows,)), dma((n_rows,)), dma((n_rows,)), dma((n_rows,)),
        dma((n_sub,)), dma((n_sub,)), dma((n_cols,)), dma((n_cols,)),
    ]
    hbm = pl.BlockSpec(memory_space=pl.ANY)
    vmem = pl.BlockSpec(memory_space=pltpu.VMEM)
    smem = pl.BlockSpec(memory_space=pltpu.SMEM)
    new_vectors, diag_out, next_columns = pl.pallas_call(
        functools.partial(kernel, (n_rows, n_cols, n_sub, hop_lead)),
        out_shape=(
            pltpu.VMEM((rows_here, batch), bf16),
            pltpu.VMEM((1, rows_here), f32),
            pltpu.VMEM((rows_here, batch), bf16),
        ),
        in_specs=[hbm, hbm, vmem, vmem, hbm, vmem, smem, smem, smem],
        out_specs=(vmem, vmem, vmem),
        scratch_shapes=scratch,
        compiler_params=pltpu.CompilerParams(
            collective_id=0, has_side_effects=True, vmem_limit_bytes=63 * 1024 * 1024),
    )(
        vectors, previous, pivots.reshape(1, batch), diagonal.reshape(1, rows_here),
        ket_blocks, tags, targets.T, counts, norms,
    )
    return new_vectors, diag_out.reshape(rows_here), next_columns


def solution(mesh):
    sizes = tuple(mesh.shape[name] for name in ("rows", "cols", "sub"))
    return jax.shard_map(
        functools.partial(body, sizes),
        mesh=mesh,
        in_specs=(
            P(("cols", "sub"), ("groups", "rows")),
            P(("groups", "rows", "cols", "sub"), None),
            P("groups"),
            P(("groups", "rows", "cols", "sub")),
            P(("groups", "rows", "cols", "sub"), None, None),
            P(("groups", "rows", "cols", "sub"), None),
            P("groups", None),
            P("groups"),
            P(),
        ),
        out_specs=(
            P(("groups", "rows", "cols", "sub"), None),
            P(("groups", "rows", "cols", "sub")),
            P(("groups", "rows", "cols", "sub"), None),
        ),
        check_vma=False,
    )
```

profile of v0, /device:TPU:0, one launch (start us, length us, event | category | flops | bytes accessed | tf_op | source)
XLA Modules:
  0.0 33.2 jit_solution(7841059162868383684)
XLA Ops:
  0.6 30.6 %shard_map.112 = (bf16[256,256]{1,0:T(8,128)(2,1)S(1)}, f32[1,256]{1,0:T(1,128)S(1)}, bf16[256,256]{1,0:T(8,128)(2,1)S(1)}) custom-call(bf16[768,1024]{1,0:T(8,128)(2,1)} %vec_hbm.1, bf16[256,256]{1,0:T(8,128)(2,1)} %prev_hbm.1, s32[1,256]{1,0:T(1,128)} %bitcast.6, f32[1,256]{1,0:T(1,128)} %bitcast.7, bf16[4,128,256]{2,1,0:T(8,128)(2,1)} %ket_hbm.1, ...), custom_call_target="tpu_custom_call" | custom-call | tf_op jit(solution)/shard_map/pallas_call | solution.py:363
  31.3 0.7 %copy.15 = bf16[256,256]{1,0:T(8,128)(2,1)} copy(bf16[256,256]{1,0:T(8,128)(2,1)S(1)} %get-tuple-element.9) | data formatting | bytes 262144
  31.9 0.6 %copy.16 = f32[256]{0:T(256)} copy(f32[256]{0:T(256)S(1)} %bitcast.4) | data formatting | bytes 2048
  32.5 0.7 %copy.17 = bf16[256,256]{1,0:T(8,128)(2,1)} copy(bf16[256,256]{1,0:T(8,128)(2,1)S(1)} %get-tuple-element.11) | data formatting | bytes 262144
where the time goes:
time: 33.3 us; the launch traced here: 33.2 us
  Pallas kernels  30.6 us (92%)
  local copies, waits for them, and re-layouts  1.88 us (6%)
  between operations  0.64 us (2%)
    pallas_call x1, Pallas kernels, body(): pl.pallas_call(functools.partial(kernel, (n_rows, n_cols, n_sub, hop_lead...  30.6 us
    unnamed x3, local copies, waits for them, and re-layouts  1.88 us

commit v1 on v0

v1 whole, which is shorter than its diff:
```python
import functools

import jax
import jax.numpy as jnp
from jax import lax
from jax.experimental import pallas as pl
from jax.experimental.pallas import tpu as pltpu
from jax.sharding import PartitionSpec as P

MESH = pl.DeviceIdType.MESH
LANES = 128
PART = 256
KET_LOW, KET_HIGH = 0, 8
REDUCE_LAG = (2, 4)
HEAD = 2
DEFER = 4
GROUPS = (2,) * 8
PD_SUB, PD_COLS = 4, 8


def column_of(row):
    return jnp.transpose(jnp.broadcast_to(row, (LANES, row.shape[1])))


def kernel(
    sizes,
    vec_hbm, prev_hbm, piv_hbm, diag_hbm, ket_hbm, tags_hbm, targets_hbm, counts_hbm, norms_hbm,
    new_ref, diag_out_ref, next_ref,
    piv_ref, diag_ref, tags_ref, targets_ref, counts_ref, norms_ref,
    vec, prev, ket, hot, own, fwd_r, fwd_l, from_l, from_r,
    pivot_t, prev_t, sub_out, sub_in, mine, col_out, col_in, scaled_t,
    stage, landed, pd_z, pd_s, pd_c, pd_own_s, pd_own_c,
    load_sem, vec_sem, zr_send, zl_send, l_recv, r_recv, sub_send, sub_recv, col_send, col_recv,
    ket_send, ket_recv, pdz_send, pdz_recv, pds_send, pds_recv, pdc_send, pdc_recv,
):
    n_rows, n_cols, n_sub, hop_lead, hop_bias, groups = sizes
    z, x, s = lax.axis_index("rows"), lax.axis_index("cols"), lax.axis_index("sub")
    column_size = n_cols * n_sub
    column = x * n_sub + s
    device = z * column_size + column
    slot_count, block_rows, batch = ket_hbm.shape
    rows_here = prev_hbm.shape[0]
    per_device = rows_here // block_rows
    width, band_rows = vec_hbm.shape
    z_chunks, z_rows = own.shape[0], own.shape[1]
    last = len(groups) - 1

    k_part = PART if width % PART == 0 else width
    load_piv = pltpu.make_async_copy(piv_hbm, piv_ref, load_sem.at[0])
    load_piv.start()
    load_diag = pltpu.make_async_copy(diag_hbm, diag_ref, load_sem.at[1])
    load_diag.start()
    load_vec = []
    for p in range(width // k_part):
        at = pl.ds(p * k_part, k_part)
        load_vec.append(pltpu.make_async_copy(vec_hbm.at[at], vec.at[at], vec_sem.at[p]))
        load_vec[-1].start()
    load_ket = pltpu.make_async_copy(ket_hbm, ket, load_sem.at[2])
    load_tags = pltpu.make_async_copy(tags_hbm, tags_ref, load_sem.at[3])
    load_targets = pltpu.make_async_copy(targets_hbm, targets_ref, load_sem.at[4])
    load_counts = pltpu.make_async_copy(counts_hbm, counts_ref, load_sem.at[5])
    load_norms = pltpu.make_async_copy(norms_hbm, norms_ref, load_sem.at[6])
    load_prev = pltpu.make_async_copy(prev_hbm, prev, load_sem.at[7])
    for c in (load_tags, load_norms, load_targets, load_counts, load_ket, load_prev):
        c.start()

    barrier = pltpu.get_barrier_semaphore()
    for name, here, count in (("rows", z, n_rows), ("cols", x, n_cols), ("sub", s, n_sub)):
        for d in range(1, count):
            pl.semaphore_signal(
                barrier, inc=1, device_id={name: lax.rem(here + d, count)}, device_id_type=MESH
            )

    load_piv.wait()
    piv_col = column_of(piv_ref[...].astype(jnp.float32)).astype(jnp.int32) - z * band_rows
    lane = lax.broadcasted_iota(jnp.int32, (batch, LANES), 1)
    for t in range(band_rows // LANES):
        hot[:, t * LANES:(t + 1) * LANES] = (piv_col == lane + t * LANES).astype(
            jnp.float32).astype(jnp.bfloat16)

    def ket_copy(d):
        return pltpu.make_async_remote_copy(
            src_ref=stage.at[d], dst_ref=landed.at[z], send_sem=ket_send.at[d],
            recv_sem=ket_recv.at[z], device_id={"rows": lax.rem(z + d, n_rows)},
            device_id_type=MESH)

    inner = (z > 0) & (z < n_rows - 1)

    def z_copy(src, dst, send, recv, q, dz):
        return pltpu.make_async_remote_copy(
            src_ref=src.at[q], dst_ref=dst.at[q], send_sem=send.at[q], recv_sem=recv.at[q],
            device_id={"rows": lax.rem(z + dz + n_rows, n_rows)}, device_id_type=MESH)

    def arrived(dst, sem):
        pltpu.make_async_remote_copy(
            src_ref=dst, dst_ref=dst, send_sem=sem, recv_sem=sem,
            device_id={"sub": lax.rem(s + 1, n_sub)}, device_id_type=MESH).wait_recv()

    load_diag.wait()
    diag_col = column_of(diag_ref[...])
    row = lax.broadcasted_iota(jnp.int32, (rows_here, LANES), 0) + device * rows_here
    for h in range(batch // LANES):
        cut = slice(h * LANES, (h + 1) * LANES)
        share = jnp.sum(jnp.where(piv_ref[:, cut] == row, diag_col, 0.0), axis=0, keepdims=True)
        pd_z[n_rows, :, cut] = share

    def pd_copies(src, dst, send, recv, name, here, count):
        return [pltpu.make_async_remote_copy(
            src_ref=src, dst_ref=dst.at[here], send_sem=send.at[d], recv_sem=recv.at[here],
            device_id={name: lax.rem(here + d, count)}, device_id_type=MESH)
            for d in range(1, count)]

    pdz = pd_copies(pd_z.at[n_rows], pd_z, pdz_send, pdz_recv, "rows", z, n_rows)
    pds = pd_copies(pd_own_s, pd_s, pds_send, pds_recv, "sub", s, n_sub)
    pdc = pd_copies(pd_own_c, pd_c, pdc_send, pdc_recv, "cols", x, n_cols)

    def gather(first, count):
        rows = slice(first * z_rows, (first + count) * z_rows)
        for p in range(width // k_part):
            if first == 0:
                load_vec[p].wait()
            at = slice(p * k_part, (p + 1) * k_part)
            got = lax.dot_general(
                hot[rows, :], vec[at, :], (((1,), (1,)), ((), ())),
                preferred_element_type=jnp.float32).astype(jnp.bfloat16)
            own[first:first + count, :, at] = got.reshape(count, z_rows, k_part)

    def send_own(first, count):
        @pl.when(z == n_rows - 1)
        def _():
            for q in range(first, first + count):
                z_copy(own, from_r, zl_send, r_recv, q, -1).start()

        @pl.when(z == 0)
        def _():
            for q in range(first, first + count):
                z_copy(own, from_l, zr_send, l_recv, q, 1).start()

    head = HEAD
    gather(0, head)
    pl.semaphore_wait(barrier, n_rows + n_cols + n_sub - 3)
    send_own(0, head)
    for c in pdz:
        c.start()
    gather(head, z_chunks - head)
    send_own(head, z_chunks - head)

    @pl.when(z == 0)
    def _():
        fwd_r[...] = own[...]

    load_tags.wait()
    load_norms.wait()
    tags = tags_ref[...]
    factor = jnp.zeros(tags.shape, jnp.float32)
    for kind in range(norms_ref.shape[0]):
        factor = jnp.where(tags == kind, norms_ref[kind], factor)
    load_ket.wait()
    for slot in range(slot_count):
        scale = column_of(factor[slot:slot + 1, :])
        for h in range(batch // LANES):
            part = (slot, slice(None), slice(h * LANES, (h + 1) * LANES))
            ket[part] = (ket[part].astype(jnp.float32) * scale).astype(jnp.bfloat16)
    load_targets.wait()
    load_counts.wait()
    used = counts_ref[device]

    def stage_for(band):
        low = (band * column_size + column) * per_device
        chosen = jnp.int32(0)
        for slot in range(slot_count):
            target = targets_ref[slot, device]
            fits = (slot < used) & (target >= low) & (target < low + per_device)
            chosen = jnp.where(fits, jnp.int32(slot), chosen)
        return ket[chosen]

    landed[z] = stage_for(z)
    for d in range(1, n_rows):
        stage[d] = stage_for(lax.rem(z + d, n_rows))

    @pl.when(inner)
    def _():
        for d in range(1, n_rows):
            ket_copy(d).start()

    def pd_total(first, dst, recv, here, count):
        total = first[...]
        for d in range(1, count):
            other = lax.rem(here + d, count)
            arrived(dst.at[other], recv.at[other])
            total = total + dst[other]
        return total

    load_prev.wait()
    prev_t[...] = jnp.transpose(prev[...].astype(jnp.float32))

    tilt = jnp.where(inner, hop_lead * (2 * z - (n_rows - 1)) + hop_bias, 0)
    wait_l = jnp.clip(tilt, 0, z_chunks)
    wait_r = jnp.clip(-tilt, 0, z_chunks)
    lag = jnp.maximum(wait_l, wait_r)
    defer = jnp.where(inner, DEFER, 0)
    reduce_lag = jnp.where(s == 0, REDUCE_LAG[0], REDUCE_LAG[1])
    def chip_rows(g):
        first, count = groups[g]
        return pl.ds(first * z_rows * n_cols, count * z_rows * n_cols)

    def group_rows(g):
        first, count = groups[g]
        return pl.ds(first * z_rows, count * z_rows)

    def sub_copy(g, d):
        return pltpu.make_async_remote_copy(
            src_ref=sub_out.at[d, chip_rows(g)], dst_ref=sub_in.at[s, chip_rows(g)],
            send_sem=sub_send.at[g, d], recv_sem=sub_recv.at[g, s],
            device_id={"sub": lax.rem(s + d, n_sub)}, device_id_type=MESH)

    def col_copy(g, d):
        return pltpu.make_async_remote_copy(
            src_ref=col_out.at[d, group_rows(g)], dst_ref=col_in.at[x, group_rows(g)],
            send_sem=col_send.at[g, d], recv_sem=col_recv.at[g, x],
            device_id={"cols": lax.rem(x + d, n_cols)}, device_id_type=MESH)

    def block_dot(pivot_rows_t, col, sub):
        at = pl.multiple_of((col * n_sub + sub) * rows_here, LANES)
        return jnp.dot(
            pivot_rows_t, vec[:, pl.ds(at, rows_here)], preferred_element_type=jnp.float32)

    def chip_part(g, c):
        first, count = groups[g]
        return pl.ds((first * n_cols + c * count) * z_rows, count * z_rows)

    def multiply(g):
        first, count = groups[g]
        chunks = slice(first, first + count)

        @pl.when(z < n_rows - 1)
        def _():
            pivot_t[chunks] = fwd_r[chunks] + from_r[chunks]

        @pl.when(z == n_rows - 1)
        def _():
            pivot_t[chunks] = fwd_r[chunks]

        pt = pivot_t[chunks].reshape(count * z_rows, width)
        for d in range(1, n_sub):
            for c in range(n_cols):
                sub_out[d, chip_part(g, c)] = block_dot(
                    pt, lax.rem(x + c, n_cols), lax.rem(s + d, n_sub))
            sub_copy(g, d).start()
        for c in range(1, n_cols):
            col_out[c, group_rows(g)] = block_dot(pt, lax.rem(x + c, n_cols), s)
        mine[group_rows(g)] = block_dot(pt, x, s)

    def reduce_chip(g):
        for d in range(1, n_sub):
            other = lax.rem(s + d, n_sub)
            arrived(sub_in.at[other, chip_rows(g)], sub_recv.at[g, other])
        for c in range(1, n_cols):
            total = col_out[c, group_rows(g)]
            for d in range(1, n_sub):
                total = total + sub_in[lax.rem(s + d, n_sub), chip_part(g, c)]
            col_out[c, group_rows(g)] = total
            col_copy(g, c).start()
        total = mine[group_rows(g)]
        for d in range(1, n_sub):
            total = total + sub_in[lax.rem(s + d, n_sub), chip_part(g, 0)]
        mine[group_rows(g)] = total

    def step(t, carry):
        q_l, q_r, q_m = t - wait_l, t - wait_r, t - lag - defer

        @pl.when((z > 0) & (q_l >= 0) & (q_l < z_chunks))
        def _():
            z_copy(fwd_r, from_l, zr_send, l_recv, q_l, 1).wait_recv()
            fwd_r[q_l] = from_l[q_l] + own[q_l]

            @pl.when(z < n_rows - 1)
            def _():
                z_copy(fwd_r, from_l, zr_send, l_recv, q_l, 1).start()

        @pl.when((z < n_rows - 1) & (q_r >= 0) & (q_r < z_chunks))
        def _():
            z_copy(fwd_l, from_r, zl_send, r_recv, q_r, -1).wait_recv()

            @pl.when(z > 0)
            def _():
                fwd_l[q_r] = from_r[q_r] + own[q_r]
                z_copy(fwd_l, from_r, zl_send, r_recv, q_r, -1).start()

        @pl.when((z == n_rows - 1) & (t == KET_HIGH))
        def _():
            for d in reversed(range(1, n_rows)):
                ket_copy(d).start()

        @pl.when((z == 0) & (t == KET_LOW))
        def _():
            for d in range(1, n_rows):
                ket_copy(d).start()

        for g in range(last + 1):
            @pl.when(q_m == sum(groups[g]) - 1)
            def _():
                multiply(g)

        for g in range(last + 1):
            @pl.when(q_m == jnp.minimum(sum(groups[g]) - 1 + reduce_lag, z_chunks - 1))
            def _():
                reduce_chip(g)

        @pl.when(t == PD_SUB)
        def _():
            pd_own_s[...] = pd_total(pd_z.at[n_rows], pd_z, pdz_recv, z, n_rows)
            for c in pds:
                c.start()

        @pl.when(t == PD_COLS)
        def _():
            pd_own_c[...] = pd_total(pd_own_s, pd_s, pds_recv, s, n_sub)
            for c in pdc:
                c.start()

        return carry

    lax.fori_loop(0, z_chunks + lag + defer, step, 0)

    pivot_diag = pd_total(pd_own_c, pd_c, pdc_recv, x, n_cols)
    inverse = 1.0 / jnp.sqrt(column_of(pivot_diag[0:1, :]))
    total_sq = jnp.zeros((1, rows_here), jnp.float32)
    written = 0
    for g in range(last + 1):
        if g == last:
            for d in range(1, n_rows):
                other = lax.rem(z + d, n_rows)
                arrived(landed.at[other], ket_recv.at[other])
            for place in range(per_device):
                block = device * per_device + place
                source = jnp.int32(0)
                for band in range(n_rows):
                    owner = band * column_size + column
                    for slot in range(slot_count):
                        fits = (slot < counts_ref[owner]) & (targets_ref[slot, owner] == block)
                        source = jnp.where(fits, jnp.int32(band), source)
                next_ref[place * block_rows:(place + 1) * block_rows, :] = landed[source]
        total = mine[group_rows(g)]
        for c in range(1, n_cols):
            other = lax.rem(x + c, n_cols)
            arrived(col_in.at[other, group_rows(g)], col_recv.at[g, other])
            total = total + col_in[other, group_rows(g)]
        first, count = groups[g]
        rows = slice(first * z_rows, (first + count) * z_rows)
        for h in range(rows_here // LANES):
            cut = slice(h * LANES, (h + 1) * LANES)
            scaled_t[rows, cut] = (prev_t[rows, cut] - total[:, cut]) * inverse[rows, :]
        scaled = scaled_t[rows, :]
        total_sq = total_sq + jnp.sum(scaled * scaled, axis=0, keepdims=True)
        ready = sum(groups[g]) * z_rows // LANES * LANES if g < last else batch
        if ready > written:
            done = slice(written, ready)
            new_ref[:, done] = jnp.transpose(scaled_t[done, :]).astype(jnp.bfloat16)
            written = ready
    diag_out_ref[...] = diag_ref[...] - total_sq

    for c in pdz + pds + pdc:
        c.wait_send()
    for d in range(1, n_rows):
        ket_copy(d).wait_send()

    @pl.when(z < n_rows - 1)
    def _():
        for q in range(z_chunks):
            z_copy(own, from_l, zr_send, l_recv, q, 1).wait_send()

    @pl.when(z > 0)
    def _():
        for q in range(z_chunks):
            z_copy(own, from_r, zl_send, r_recv, q, -1).wait_send()

    for g in range(last + 1):
        for d in range(1, n_sub):
            sub_copy(g, d).wait_send()
        for c in range(1, n_cols):
            col_copy(g, c).wait_send()


def flush(new_ref, diag_ref, next_ref, new_hbm, diag_hbm, next_hbm, sem):
    copies = [
        pltpu.make_async_copy(new_ref, new_hbm, sem.at[0]),
        pltpu.make_async_copy(next_ref, next_hbm, sem.at[1]),
        pltpu.make_async_copy(diag_ref, diag_hbm, sem.at[2]),
    ]
    for c in copies:
        c.start()
    for c in copies:
        c.wait()


def body(mesh_sizes, vectors, previous, pivots, diagonal, ket_blocks, tags, targets, counts, norms):
    n_rows, n_cols, n_sub = mesh_sizes
    width, band_rows = vectors.shape
    rows_here, batch = previous.shape
    slot_count, block_rows, _ = ket_blocks.shape
    z_chunks, hop_lead, hop_bias = 16, 6, 1
    z_rows, m_chunks = batch // z_chunks, len(GROUPS)
    groups = tuple((sum(GROUPS[:g]), GROUPS[g]) for g in range(m_chunks))
    f32, bf16, dma = jnp.float32, jnp.bfloat16, pltpu.SemaphoreType.DMA
    line = pltpu.VMEM((z_chunks, z_rows, width), bf16)
    small = pltpu.VMEM((1, batch), f32)
    scratch = [
        pltpu.VMEM((1, batch), jnp.int32), pltpu.VMEM((1, rows_here), f32),
        pltpu.VMEM(tags.shape, jnp.int32), pltpu.SMEM(targets.shape[::-1], jnp.int32),
        pltpu.SMEM(counts.shape, jnp.int32), pltpu.SMEM(norms.shape, f32),
        pltpu.VMEM(vectors.shape, bf16), pltpu.VMEM(previous.shape, bf16),
        pltpu.VMEM(ket_blocks.shape, bf16), pltpu.VMEM((batch, band_rows), bf16),
        line, line, line, line, line, line,
        pltpu.VMEM((batch, rows_here), f32),
        pltpu.VMEM((n_sub, n_cols * batch, rows_here), f32),
        pltpu.VMEM((n_sub, n_cols * batch, rows_here), f32),
        pltpu.VMEM((batch, rows_here), f32),
        pltpu.VMEM((n_cols, batch, rows_here), f32),
        pltpu.VMEM((n_cols, batch, rows_here), f32),
        pltpu.VMEM((batch, rows_here), f32),
        pltpu.VMEM((n_rows, block_rows, batch), bf16),
        pltpu.VMEM((n_rows, block_rows, batch), bf16),
        pltpu.VMEM((n_rows + 1, 1, batch), f32), pltpu.VMEM((n_sub, 1, batch), f32),
        pltpu.VMEM((n_cols, 1, batch), f32), small, small,
        dma((8,)), dma((max(width // PART, 1),)), dma((z_chunks,)), dma((z_chunks,)), dma((z_chunks,)), dma((z_chunks,)),
        dma((m_chunks, n_sub)), dma((m_chunks, n_sub)),
        dma((m_chunks, n_cols)), dma((m_chunks, n_cols)),
        dma((n_rows,)), dma((n_rows,)), dma((n_rows,)), dma((n_rows,)),
        dma((n_sub,)), dma((n_sub,)), dma((n_cols,)), dma((n_cols,)),
    ]
    hbm = pl.BlockSpec(memory_space=pl.ANY)
    vmem = pl.BlockSpec(memory_space=pltpu.VMEM)
    new_vectors, diag_out, next_columns = pl.pallas_call(
        functools.partial(kernel, (n_rows, n_cols, n_sub, hop_lead, hop_bias, groups)),
        out_shape=(
            pltpu.VMEM((rows_here, batch), bf16),
            pltpu.VMEM((1, rows_here), f32),
            pltpu.VMEM((rows_here, batch), bf16),
        ),
        in_specs=[hbm] * 9,
        out_specs=(vmem, vmem, vmem),
        scratch_shapes=scratch,
        compiler_params=pltpu.CompilerParams(
            collective_id=0, has_side_effects=True, vmem_limit_bytes=63 * 1024 * 1024),
    )(
        vectors, previous, pivots.reshape(1, batch), diagonal.reshape(1, rows_here),
        ket_blocks, tags, targets.T, counts, norms,
    )
    new_vectors, diag_out, next_columns = pl.pallas_call(
        flush,
        out_shape=(
            jax.ShapeDtypeStruct((rows_here, batch), bf16),
            jax.ShapeDtypeStruct((1, rows_here), f32),
            jax.ShapeDtypeStruct((rows_here, batch), bf16),
        ),
        in_specs=[vmem] * 3,
        out_specs=(hbm, hbm, hbm),
        scratch_shapes=[dma((3,))],
        compiler_params=pltpu.CompilerParams(vmem_limit_bytes=1024 * 1024),
    )(new_vectors, diag_out, next_columns)
    return new_vectors, diag_out.reshape(rows_here), next_columns


def solution(mesh):
    sizes = tuple(mesh.shape[name] for name in ("rows", "cols", "sub"))
    return jax.shard_map(
        functools.partial(body, sizes),
        mesh=mesh,
        in_specs=(
            P(("cols", "sub"), ("groups", "rows")),
            P(("groups", "rows", "cols", "sub"), None),
            P("groups"),
            P(("groups", "rows", "cols", "sub")),
            P(("groups", "rows", "cols", "sub"), None, None),
            P(("groups", "rows", "cols", "sub"), None),
            P("groups", None),
            P("groups"),
            P(),
        ),
        out_specs=(
            P(("groups", "rows", "cols", "sub"), None),
            P(("groups", "rows", "cols", "sub")),
            P(("groups", "rows", "cols", "sub"), None),
        ),
        check_vma=False,
    )
```

time: 33.3 us -> 30 us (0.901)
  local copies, waits for them, and re-layouts: 1.88 us -> 0 us
  Pallas kernels: 30.6 us -> 29.2 us
    pallas_call x1, Pallas kernels: 30.6 us -> 28.5 us  [body(): pl.pallas_call(functools.partial(kernel, (n_rows, n_cols, n_sub, hop_lead...]
    unnamed x3 -> x0, local copies, waits for them, and re-layouts: 1.88 us -> none
    pallas_call x0 -> x1, Pallas kernels: none -> 0.73 us  [body(): pl.pallas_call(flush, out_shape=(jax.ShapeDtypeStruct((rows_here, batch),...]
where the time goes in v1:
time: 30 us; the launch traced here: 29.9 us
  Pallas kernels  29.2 us (97%)
  between operations  0.64 us (2%)
    pallas_call x1, Pallas kernels, body(): pl.pallas_call(functools.partial(kernel, (n_rows, n_cols, n_sub, hop_lead...  28.5 us
    pallas_call x1, Pallas kernels, body(): pl.pallas_call(flush, out_shape=(jax.ShapeDtypeStruct((rows_here, batch),...  0.73 us

profile of v1, /device:TPU:0, one launch (start us, length us, event | category | flops | bytes accessed | tf_op | source)
XLA Modules:
  0.0 29.9 jit_solution(12426634783241523718)
XLA Ops:
  0.6 28.5 %shard_map.112 = (bf16[256,256]{1,0:T(8,128)(2,1)S(1)}, f32[1,256]{1,0:T(1,128)S(1)}, bf16[256,256]{1,0:T(8,128)(2,1)S(1)}) custom-call(bf16[768,1024]{1,0:T(8,128)(2,1)} %vec_hbm.1, bf16[256,256]{1,0:T(8,128)(2,1)} %prev_hbm.1, s32[1,256]{1,0:T(1,128)} %bitcast.5, f32[1,256]{1,0:T(1,128)} %bitcast.6, bf16[4,128,256]{2,1,0:T(8,128)(2,1)} %ket_hbm.1, ...), custom_call_target="tpu_custom_call" | custom-call | tf_op jit(solution)/shard_map/pallas_call | solution.py:434
  29.1 0.7 %shard_map.113 = (bf16[256,256]{1,0:T(8,128)(2,1)}, f32[1,256]{1,0:T(1,128)}, bf16[256,256]{1,0:T(8,128)(2,1)}) custom-call(bf16[256,256]{1,0:T(8,128)(2,1)S(1)} %get-tuple-element.9.new_ref, f32[1,256]{1,0:T(1,128)S(1)} %get-tuple-element.10.diag_ref, bf16[256,256]{1,0:T(8,128)(2,1)S(1)} %get-tuple-element.11.next_ref), custom_call_target="tpu_custom_call" | custom-call | tf_op jit(solution)/shard_map/pallas_call | solution.py:450

commit v2 on v1

--- a/solution.py
+++ b/solution.py
@@ -10,11 +10,11 @@
 MESH = pl.DeviceIdType.MESH
 LANES = 128
 PART = 256
-KET_LOW, KET_HIGH = 0, 8
-REDUCE_LAG = (2, 4)
+KET_LOW, KET_HIGH = (0, 2), (4, 3)
+REDUCE_LAG = (1, 5)
 HEAD = 2
 DEFER = 4
-GROUPS = (2,) * 8
+PER = 2
 PD_SUB, PD_COLS = 4, 8
 
 
@@ -28,12 +28,12 @@
     new_ref, diag_out_ref, next_ref,
     piv_ref, diag_ref, tags_ref, targets_ref, counts_ref, norms_ref,
     vec, prev, ket, hot, own, fwd_r, fwd_l, from_l, from_r,
-    pivot_t, prev_t, sub_out, sub_in, mine, col_out, col_in, scaled_t,
+    pivot_t, prev_t, sub_out, sub_in, mine, col_out, col_in, scaled_t, inverse,
     stage, landed, pd_z, pd_s, pd_c, pd_own_s, pd_own_c,
     load_sem, vec_sem, zr_send, zl_send, l_recv, r_recv, sub_send, sub_recv, col_send, col_recv,
     ket_send, ket_recv, pdz_send, pdz_recv, pds_send, pds_recv, pdc_send, pdc_recv,
 ):
-    n_rows, n_cols, n_sub, hop_lead, hop_bias, groups = sizes
+    n_rows, n_cols, n_sub, hop_lead, hop_bias, per = sizes
     z, x, s = lax.axis_index("rows"), lax.axis_index("cols"), lax.axis_index("sub")
     column_size = n_cols * n_sub
     column = x * n_sub + s
@@ -43,7 +43,9 @@
     per_device = rows_here // block_rows
     width, band_rows = vec_hbm.shape
     z_chunks, z_rows = own.shape[0], own.shape[1]
-    last = len(groups) - 1
+    groups = z_chunks // per
+    last = groups - 1
+    g_rows = per * z_rows
 
     k_part = PART if width % PART == 0 else width
     load_piv = pltpu.make_async_copy(piv_hbm, piv_ref, load_sem.at[0])
@@ -201,12 +203,10 @@
     defer = jnp.where(inner, DEFER, 0)
     reduce_lag = jnp.where(s == 0, REDUCE_LAG[0], REDUCE_LAG[1])
     def chip_rows(g):
-        first, count = groups[g]
-        return pl.ds(first * z_rows * n_cols, count * z_rows * n_cols)
+        return pl.ds(pl.multiple_of(g * g_rows * n_cols, 8), g_rows * n_cols)
 
     def group_rows(g):
-        first, count = groups[g]
-        return pl.ds(first * z_rows, count * z_rows)
+        return pl.ds(pl.multiple_of(g * g_rows, 8), g_rows)
 
     def sub_copy(g, d):
         return pltpu.make_async_remote_copy(
@@ -226,12 +226,10 @@
             pivot_rows_t, vec[:, pl.ds(at, rows_here)], preferred_element_type=jnp.float32)
 
     def chip_part(g, c):
-        first, count = groups[g]
-        return pl.ds((first * n_cols + c * count) * z_rows, count * z_rows)
+        return pl.ds(pl.multiple_of((g * n_cols + c) * g_rows, 8), g_rows)
 
     def multiply(g):
-        first, count = groups[g]
-        chunks = slice(first, first + count)
+        chunks = pl.ds(g * per, per)
 
         @pl.when(z < n_rows - 1)
         def _():
@@ -241,7 +239,7 @@
         def _():
             pivot_t[chunks] = fwd_r[chunks]
 
-        pt = pivot_t[chunks].reshape(count * z_rows, width)
+        pt = pivot_t[chunks].reshape(g_rows, width)
         for d in range(1, n_sub):
             for c in range(n_cols):
                 sub_out[d, chip_part(g, c)] = block_dot(
@@ -287,25 +285,27 @@
                 fwd_l[q_r] = from_r[q_r] + own[q_r]
                 z_copy(fwd_l, from_r, zl_send, r_recv, q_r, -1).start()
 
-        @pl.when((z == n_rows - 1) & (t == KET_HIGH))
-        def _():
-            for d in reversed(range(1, n_rows)):
-                ket_copy(d).start()
-
-        @pl.when((z == 0) & (t == KET_LOW))
-        def _():
-            for d in range(1, n_rows):
-                ket_copy(d).start()
-
-        for g in range(last + 1):
-            @pl.when(q_m == sum(groups[g]) - 1)
+        for far in range(1, n_rows):
+            low_at = min(KET_LOW[0] + (far - 1) * KET_LOW[1], z_chunks - 1)
+            high_at = min(KET_HIGH[0] + (far - 1) * KET_HIGH[1], z_chunks - 1)
+
+            @pl.when((z == 0) & (t == low_at))
             def _():
-                multiply(g)
-
-        for g in range(last + 1):
-            @pl.when(q_m == jnp.minimum(sum(groups[g]) - 1 + reduce_lag, z_chunks - 1))
+                ket_copy(far).start()
+
+            @pl.when((z == n_rows - 1) & (t == high_at))
             def _():
-                reduce_chip(g)
+                ket_copy(n_rows - far).start()
+
+        @pl.when((q_m >= 0) & (lax.rem(q_m, per) == per - 1))
+        def _():
+            multiply(q_m // per)
+
+        q_e = q_m - reduce_lag + 1
+
+        @pl.when((q_e >= per) & (q_m < z_chunks - 1) & (lax.rem(q_e, per) == 0))
+        def _():
+            reduce_chip(q_e // per - 1)
 
         @pl.when(t == PD_SUB)
         def _():
@@ -323,42 +323,58 @@
 
     lax.fori_loop(0, z_chunks + lag + defer, step, 0)
 
+    def reduce_rest(g, carry):
+        reduce_chip(g)
+        return carry
+
+    lax.fori_loop((z_chunks - 1 - reduce_lag) // per, groups, reduce_rest, 0)
+
     pivot_diag = pd_total(pd_own_c, pd_c, pdc_recv, x, n_cols)
-    inverse = 1.0 / jnp.sqrt(column_of(pivot_diag[0:1, :]))
-    total_sq = jnp.zeros((1, rows_here), jnp.float32)
-    written = 0
-    for g in range(last + 1):
-        if g == last:
-            for d in range(1, n_rows):
-                other = lax.rem(z + d, n_rows)
-                arrived(landed.at[other], ket_recv.at[other])
-            for place in range(per_device):
-                block = device * per_device + place
-                source = jnp.int32(0)
-                for band in range(n_rows):
-                    owner = band * column_size + column
-                    for slot in range(slot_count):
-                        fits = (slot < counts_ref[owner]) & (targets_ref[slot, owner] == block)
-                        source = jnp.where(fits, jnp.int32(band), source)
-                next_ref[place * block_rows:(place + 1) * block_rows, :] = landed[source]
+    inverse[...] = 1.0 / jnp.sqrt(column_of(pivot_diag[0:1, :]))
+    def each(count, wait):
+        def one(q, carry):
+            wait(q)
+            return carry
+
+        lax.fori_loop(0, count, one, 0)
+
+    def finish(g, total_sq):
         total = mine[group_rows(g)]
         for c in range(1, n_cols):
             other = lax.rem(x + c, n_cols)
             arrived(col_in.at[other, group_rows(g)], col_recv.at[g, other])
             total = total + col_in[other, group_rows(g)]
-        first, count = groups[g]
-        rows = slice(first * z_rows, (first + count) * z_rows)
+        rows = group_rows(g)
+        scale = inverse[rows, :]
         for h in range(rows_here // LANES):
             cut = slice(h * LANES, (h + 1) * LANES)
-            scaled_t[rows, cut] = (prev_t[rows, cut] - total[:, cut]) * inverse[rows, :]
+            scaled_t[rows, cut] = (prev_t[rows, cut] - total[:, cut]) * scale
         scaled = scaled_t[rows, :]
-        total_sq = total_sq + jnp.sum(scaled * scaled, axis=0, keepdims=True)
-        ready = sum(groups[g]) * z_rows // LANES * LANES if g < last else batch
-        if ready > written:
-            done = slice(written, ready)
-            new_ref[:, done] = jnp.transpose(scaled_t[done, :]).astype(jnp.bfloat16)
-            written = ready
-    diag_out_ref[...] = diag_ref[...] - total_sq
+        return total_sq + jnp.sum(scaled * scaled, axis=0, keepdims=True)
+
+    def write(first, count):
+        done = slice(first, first + count)
+        new_ref[:, done] = jnp.transpose(scaled_t[done, :]).astype(jnp.bfloat16)
+
+    total_sq = jnp.zeros((1, rows_here), jnp.float32)
+    early = (batch - 1) // LANES * LANES // g_rows
+    total_sq = lax.fori_loop(0, early, finish, total_sq)
+    if early:
+        write(0, early * g_rows)
+    total_sq = lax.fori_loop(early, last, finish, total_sq)
+
+    for d in range(1, n_rows):
+        other = lax.rem(z + d, n_rows)
+        arrived(landed.at[other], ket_recv.at[other])
+    for place in range(per_device):
+        block = device * per_device + place
+        source = jnp.int32(0)
+        for band in range(n_rows):
+            owner = band * column_size + column
+            for slot in range(slot_count):
+                fits = (slot < counts_ref[owner]) & (targets_ref[slot, owner] == block)
+                source = jnp.where(fits, jnp.int32(band), source)
+        next_ref[place * block_rows:(place + 1) * block_rows, :] = landed[source]
 
     for c in pdz + pds + pdc:
         c.wait_send()
@@ -367,19 +383,22 @@
 
     @pl.when(z < n_rows - 1)
     def _():
-        for q in range(z_chunks):
-            z_copy(own, from_l, zr_send, l_recv, q, 1).wait_send()
+        each(z_chunks, lambda q: z_copy(own, from_l, zr_send, l_recv, q, 1).wait_send())
 
     @pl.when(z > 0)
     def _():
-        for q in range(z_chunks):
-            z_copy(own, from_r, zl_send, r_recv, q, -1).wait_send()
-
-    for g in range(last + 1):
-        for d in range(1, n_sub):
-            sub_copy(g, d).wait_send()
-        for c in range(1, n_cols):
-            col_copy(g, c).wait_send()
+        each(z_chunks, lambda q: z_copy(own, from_r, zl_send, r_recv, q, -1).wait_send())
+
+    for d in range(1, n_sub):
+        each(groups, lambda g: sub_copy(g, d).wait_send())
+    for c in range(1, n_cols):
+        each(last, lambda g: col_copy(g, c).wait_send())
+
+    total_sq = finish(last, total_sq)
+    write(early * g_rows, batch - early * g_rows)
+    diag_out_ref[...] = diag_ref[...] - total_sq
+    for c in range(1, n_cols):
+        col_copy(last, c).wait_send()
 
 
 def flush(new_ref, diag_ref, next_ref, new_hbm, diag_hbm, next_hbm, sem):
@@ -400,8 +419,7 @@
     rows_here, batch = previous.shape
     slot_count, block_rows, _ = ket_blocks.shape
     z_chunks, hop_lead, hop_bias = 16, 6, 1
-    z_rows, m_chunks = batch // z_chunks, len(GROUPS)
-    groups = tuple((sum(GROUPS[:g]), GROUPS[g]) for g in range(m_chunks))
+    z_rows, m_chunks = batch // z_chunks, z_chunks // PER
     f32, bf16, dma = jnp.float32, jnp.bfloat16, pltpu.SemaphoreType.DMA
     line = pltpu.VMEM((z_chunks, z_rows, width), bf16)
     small = pltpu.VMEM((1, batch), f32)
@@ -418,7 +436,7 @@
         pltpu.VMEM((batch, rows_here), f32),
         pltpu.VMEM((n_cols, batch, rows_here), f32),
         pltpu.VMEM((n_cols, batch, rows_here), f32),
-        pltpu.VMEM((batch, rows_here), f32),
+        pltpu.VMEM((batch, rows_here), f32), pltpu.VMEM((batch, LANES), f32),
         pltpu.VMEM((n_rows, block_rows, batch), bf16),
         pltpu.VMEM((n_rows, block_rows, batch), bf16),
         pltpu.VMEM((n_rows + 1, 1, batch), f32), pltpu.VMEM((n_sub, 1, batch), f32),
@@ -432,7 +450,7 @@
     hbm = pl.BlockSpec(memory_space=pl.ANY)
     vmem = pl.BlockSpec(memory_space=pltpu.VMEM)
     new_vectors, diag_out, next_columns = pl.pallas_call(
-        functools.partial(kernel, (n_rows, n_cols, n_sub, hop_lead, hop_bias, groups)),
+        functools.partial(kernel, (n_rows, n_cols, n_sub, hop_lead, hop_bias, PER)),
         out_shape=(
             pltpu.VMEM((rows_here, batch), bf16),
             pltpu.VMEM((1, rows_here), f32),

time: 30 us -> 29.2 us (0.973)
  Pallas kernels: 29.2 us -> 28.4 us
    pallas_call x1, Pallas kernels: 28.5 us -> 27.7 us  [body(): pl.pallas_call(functools.partial(kernel, (n_rows, n_cols, n_sub, hop_lead...]
where the time goes in v2:
time: 29.2 us; the launch traced here: 29 us
  Pallas kernels  28.4 us (97%)
  between operations  0.64 us (2%)
    pallas_call x1, Pallas kernels, body(): pl.pallas_call(functools.partial(kernel, (n_rows, n_cols, n_sub, hop_lead...  27.7 us
    pallas_call x1, Pallas kernels, body(): pl.pallas_call(flush, out_shape=(jax.ShapeDtypeStruct((rows_here, batch),...  0.73 us

profile of v2, /device:TPU:0, one launch (start us, length us, event | category | flops | bytes accessed | tf_op | source)
XLA Modules:
  0.0 29.0 jit_solution(9331894356951572908)
XLA Ops:
  0.6 27.7 %shard_map.112 = (bf16[256,256]{1,0:T(8,128)(2,1)S(1)}, f32[1,256]{1,0:T(1,128)S(1)}, bf16[256,256]{1,0:T(8,128)(2,1)S(1)}) custom-call(bf16[768,1024]{1,0:T(8,128)(2,1)} %vec_hbm.1, bf16[256,256]{1,0:T(8,128)(2,1)} %prev_hbm.1, s32[1,256]{1,0:T(1,128)} %bitcast.5, f32[1,256]{1,0:T(1,128)} %bitcast.6, bf16[4,128,256]{2,1,0:T(8,128)(2,1)} %ket_hbm.1, ...), custom_call_target="tpu_custom_call" | custom-call | tf_op jit(solution)/shard_map/pallas_call | solution.py:452
  28.3 0.7 %shard_map.113 = (bf16[256,256]{1,0:T(8,128)(2,1)}, f32[1,256]{1,0:T(1,128)}, bf16[256,256]{1,0:T(8,128)(2,1)}) custom-call(bf16[256,256]{1,0:T(8,128)(2,1)S(1)} %get-tuple-element.9.new_ref, f32[1,256]{1,0:T(1,128)S(1)} %get-tuple-element.10.diag_ref, bf16[256,256]{1,0:T(8,128)(2,1)S(1)} %get-tuple-element.11.next_ref), custom_call_target="tpu_custom_call" | custom-call | tf_op jit(solution)/shard_map/pallas_call | solution.py:468

commit v3 on v2

--- a/solution.py
+++ b/solution.py
@@ -63,7 +63,7 @@
     load_counts = pltpu.make_async_copy(counts_hbm, counts_ref, load_sem.at[5])
     load_norms = pltpu.make_async_copy(norms_hbm, norms_ref, load_sem.at[6])
     load_prev = pltpu.make_async_copy(prev_hbm, prev, load_sem.at[7])
-    for c in (load_tags, load_norms, load_targets, load_counts, load_ket, load_prev):
+    for c in (load_tags, load_norms, load_targets, load_counts):
         c.start()
 
     barrier = pltpu.get_barrier_semaphore()
@@ -140,11 +140,13 @@
 
     head = HEAD
     gather(0, head)
+    load_ket.start()
+    load_prev.start()
     pl.semaphore_wait(barrier, n_rows + n_cols + n_sub - 3)
     send_own(0, head)
+    gather(head, z_chunks - head)
     for c in pdz:
         c.start()
-    gather(head, z_chunks - head)
     send_own(head, z_chunks - head)
 
     @pl.when(z == 0)
@@ -196,7 +198,8 @@
     load_prev.wait()
     prev_t[...] = jnp.transpose(prev[...].astype(jnp.float32))
 
-    tilt = jnp.where(inner, hop_lead * (2 * z - (n_rows - 1)) + hop_bias, 0)
+    lead = jnp.where(s == 0, hop_lead[0], hop_lead[1])
+    tilt = jnp.where(inner, lead * (2 * z - (n_rows - 1)) + hop_bias, 0)
     wait_l = jnp.clip(tilt, 0, z_chunks)
     wait_r = jnp.clip(-tilt, 0, z_chunks)
     lag = jnp.maximum(wait_l, wait_r)
@@ -418,7 +421,7 @@
     width, band_rows = vectors.shape
     rows_here, batch = previous.shape
     slot_count, block_rows, _ = ket_blocks.shape
-    z_chunks, hop_lead, hop_bias = 16, 6, 1
+    z_chunks, hop_lead, hop_bias = 16, (7, 5), 1
     z_rows, m_chunks = batch // z_chunks, z_chunks // PER
     f32, bf16, dma = jnp.float32, jnp.bfloat16, pltpu.SemaphoreType.DMA
     line = pltpu.VMEM((z_chunks, z_rows, width), bf16)

time: 29.2 us -> 29.1 us (level)
  no operation moved by 1% of the time
where the time goes in v3:
time: 29.1 us; the launch traced here: 28.9 us
  Pallas kernels  28.2 us (97%)
  between operations  0.64 us (2%)
    pallas_call x1, Pallas kernels, body(): pl.pallas_call(functools.partial(kernel, (n_rows, n_cols, n_sub, hop_lead...  27.5 us
    pallas_call x1, Pallas kernels, body(): pl.pallas_call(flush, out_shape=(jax.ShapeDtypeStruct((rows_here, batch),...  0.73 us

profile of v3, /device:TPU:0, one launch (start us, length us, event | category | flops | bytes accessed | tf_op | source)
XLA Modules:
  0.0 28.9 jit_solution(17310561545720477902)
XLA Ops:
  0.6 27.5 %shard_map.112 = (bf16[256,256]{1,0:T(8,128)(2,1)S(1)}, f32[1,256]{1,0:T(1,128)S(1)}, bf16[256,256]{1,0:T(8,128)(2,1)S(1)}) custom-call(bf16[768,1024]{1,0:T(8,128)(2,1)} %vec_hbm.1, bf16[256,256]{1,0:T(8,128)(2,1)} %prev_hbm.1, s32[1,256]{1,0:T(1,128)} %bitcast.5, f32[1,256]{1,0:T(1,128)} %bitcast.6, bf16[4,128,256]{2,1,0:T(8,128)(2,1)} %ket_hbm.1, ...), custom_call_target="tpu_custom_call" | custom-call | tf_op jit(solution)/shard_map/pallas_call | solution.py:455
  28.2 0.7 %shard_map.113 = (bf16[256,256]{1,0:T(8,128)(2,1)}, f32[1,256]{1,0:T(1,128)}, bf16[256,256]{1,0:T(8,128)(2,1)}) custom-call(bf16[256,256]{1,0:T(8,128)(2,1)S(1)} %get-tuple-element.9.new_ref, f32[1,256]{1,0:T(1,128)S(1)} %get-tuple-element.10.diag_ref, bf16[256,256]{1,0:T(8,128)(2,1)S(1)} %get-tuple-element.11.next_ref), custom_call_target="tpu_custom_call" | custom-call | tf_op jit(solution)/shard_map/pallas_call | solution.py:471

commit v4 on v3

--- a/solution.py
+++ b/solution.py
@@ -53,10 +53,8 @@
     load_diag = pltpu.make_async_copy(diag_hbm, diag_ref, load_sem.at[1])
     load_diag.start()
     load_vec = []
-    for p in range(width // k_part):
-        at = pl.ds(p * k_part, k_part)
-        load_vec.append(pltpu.make_async_copy(vec_hbm.at[at], vec.at[at], vec_sem.at[p]))
-        load_vec[-1].start()
+    load_vec.append(pltpu.make_async_copy(vec_hbm, vec, vec_sem.at[0]))
+    load_vec[-1].start()
     load_ket = pltpu.make_async_copy(ket_hbm, ket, load_sem.at[2])
     load_tags = pltpu.make_async_copy(tags_hbm, tags_ref, load_sem.at[3])
     load_targets = pltpu.make_async_copy(targets_hbm, targets_ref, load_sem.at[4])
@@ -119,7 +117,7 @@
     def gather(first, count):
         rows = slice(first * z_rows, (first + count) * z_rows)
         for p in range(width // k_part):
-            if first == 0:
+            if first == 0 and p == 0:
                 load_vec[p].wait()
             at = slice(p * k_part, (p + 1) * k_part)
             got = lax.dot_general(

time: 29.1 us -> 28.9 us (level)
  no operation moved by 1% of the time
where the time goes in v4:
time: 28.9 us; the launch traced here: 28.8 us
  Pallas kernels  28.1 us (97%)
  between operations  0.64 us (2%)
    pallas_call x1, Pallas kernels, body(): pl.pallas_call(functools.partial(kernel, (n_rows, n_cols, n_sub, hop_lead...  27.4 us
    pallas_call x1, Pallas kernels, body(): pl.pallas_call(flush, out_shape=(jax.ShapeDtypeStruct((rows_here, batch),...  0.73 us

profile of v4, /device:TPU:0, one launch (start us, length us, event | category | flops | bytes accessed | tf_op | source)
XLA Modules:
  0.0 28.8 jit_solution(7579521778093786967)
XLA Ops:
  0.6 27.4 %shard_map.112 = (bf16[256,256]{1,0:T(8,128)(2,1)S(1)}, f32[1,256]{1,0:T(1,128)S(1)}, bf16[256,256]{1,0:T(8,128)(2,1)S(1)}) custom-call(bf16[768,1024]{1,0:T(8,128)(2,1)} %vec_hbm.1, bf16[256,256]{1,0:T(8,128)(2,1)} %prev_hbm.1, s32[1,256]{1,0:T(1,128)} %bitcast.5, f32[1,256]{1,0:T(1,128)} %bitcast.6, bf16[4,128,256]{2,1,0:T(8,128)(2,1)} %ket_hbm.1, ...), custom_call_target="tpu_custom_call" | custom-call | tf_op jit(solution)/shard_map/pallas_call | solution.py:453
  28.0 0.7 %shard_map.113 = (bf16[256,256]{1,0:T(8,128)(2,1)}, f32[1,256]{1,0:T(1,128)}, bf16[256,256]{1,0:T(8,128)(2,1)}) custom-call(bf16[256,256]{1,0:T(8,128)(2,1)S(1)} %get-tuple-element.9.new_ref, f32[1,256]{1,0:T(1,128)S(1)} %get-tuple-element.10.diag_ref, bf16[256,256]{1,0:T(8,128)(2,1)S(1)} %get-tuple-element.11.next_ref), custom_call_target="tpu_custom_call" | custom-call | tf_op jit(solution)/shard_map/pallas_call | solution.py:469
